TPU v7x, 32 devices: a whole 2x2x4 slice. The times are simulated.
32 devices in a mesh: path: 16 (over z, x, core), shard: 2 (over y).
Axes of the slice: x: 2, y: 2, z: 4, core: 2. Of those that a mesh axis runs over, the one named last changes fastest.
Arguments:
- deltas: bfloat16 [16, 32, 4096], P('path', 'shard'), may hold values from -96 to 96
- momentum: float32 [16, 32, 4096], P(None, 'shard', 'path'), may hold values from -4 to 4
- path_module: int32 [16], replicated, may hold values from 0 to 15, as said below
Outputs:
- path_update: bfloat16 [16, 32, 4096], P('path', 'shard')
- new_momentum: float32 [16, 32, 4096], P(None, 'shard', 'path')
Inputs may be any that keep to these rules, and one draw needn't show every extreme that they name: `path_module`: every module is used by at least one and at most seven paths.
All inputs are finite; a program needn't handle non-finite values.
Results may differ from a plain program's by a relative error of at most 0.0004.
Values may be sent and summed in bfloat16 or wider, within the bound.
A program may use at most 64 MiB of HBM per device.

v0:
```python
import jax
import jax.numpy as jnp
from jax import lax
from jax.sharding import PartitionSpec as P

D = 4096
outer_rate = 0.7
momentum_rate = 0.9
clip_ratio = 2.0


def local(deltas, momentum, path_module):
    own_index = lax.axis_index("path")
    modules = momentum.shape[0]
    row_count = deltas.shape[1]
    onehot = (path_module[:, None] == jnp.arange(modules, dtype=jnp.int32)[None, :]).astype(
        jnp.float32
    )
    counts = jnp.sum(onehot, axis=0)
    own_module = lax.dynamic_index_in_dim(path_module, own_index, 0, keepdims=False)
    column_pieces = lax.all_to_all(deltas, "path", split_axis=2, concat_axis=0, tiled=True)
    totals = jnp.einsum(
        "pm,prc->mrc",
        onehot.astype(jnp.bfloat16),
        column_pieces,
        preferred_element_type=jnp.float32,
    )
    outer_grad = totals / counts[:, None, None]
    local_squares = jnp.sum(outer_grad * outer_grad, axis=(1, 2))
    norm_squares = lax.psum(local_squares, ("path", "shard"))
    limit = clip_ratio * jnp.sqrt(jnp.float32(row_count * lax.axis_size("shard") * D))
    shrink = jnp.minimum(1.0, limit / jnp.sqrt(norm_squares + 1e-06))
    clipped = outer_grad * shrink[:, None, None]
    new_momentum = momentum_rate * momentum + clipped
    outer_step = (outer_rate * (clipped + momentum_rate * new_momentum)).astype(jnp.bfloat16)
    gathered = lax.all_gather(outer_step, "path", axis=2, tiled=True)
    path_update = lax.dynamic_index_in_dim(gathered, own_module, 0, keepdims=True)
    return (path_update, new_momentum)


def solution(mesh):
    return jax.shard_map(
        local,
        mesh=mesh,
        in_specs=(P("path", "shard", None), P(None, "shard", "path"), P()),
        out_specs=(P("path", "shard", None), P(None, "shard", "path")),
        check_vma=False,
    )
```

profile of v0, /device:TPU:0, one launch (start us, length us, event | category | flops | bytes accessed | tf_op | source)
XLA Modules:
  0.0 145.2 jit_solution(7055501070345371449)
XLA Ops:
  7.2 4.3 %copy.8 = bf16[1,16,4096]{1,0,2:T(2,128)(2,1)S(1)} copy(bf16[1,16,4096]{2,1,0:T(8,128)(2,1)} %param.3) | data formatting | bytes 262144 | tf_op args[0]
  11.5 0.5 broadcast.26
  12.0 0.0 copy-start.1
  12.0 22.4 %reduce = bf16[4096,16]{1,0:T(8,128)(2,1)S(1)} reduce(bf16[4096,1,16]{2,1,0:T(2,128)(2,1)S(1)} %bitcast.25, bf16[]{:T(256)} %broadcast.26), dimensions={1}, to_apply=%bitcast.15.reduce_sub_computation | reduce | bytes 262146
  34.4 1.8 %reshape.8 = bf16[16,2,2048]{2,1,0:T(2,128)(2,1)} reshape(bf16[4096,16]{1,0:T(8,128)(2,1)S(1)} %reduce) | data formatting | bytes 262144
  36.2 7.4 %all-to-all-start = ((bf16[16,2,2048]{2,1,0:T(2,128)(2,1)}), bf16[16,2,2048]{2,1,0:T(2,128)(2,1)S(1)}, u32[]{:S(2)}, u32[]{:S(2)}) async-start(bf16[16,2,2048]{2,1,0:T(2,128)(2,1)} %reshape.8), calls=%async_computation | async-start | bytes 262144 | tf_op jit(solution)/shard_map/all_to_all | solution.py:21
  43.6 0.0 all-gather.2.cloned.1.call-start
  43.6 0.0 copy-done.1
  43.6 0.1 convert_reduce_fusion
  43.8 7.7 %all-to-all-done = bf16[16,2,2048]{2,1,0:T(2,128)(2,1)S(1)} async-done(((bf16[16,2,2048]{2,1,0:T(2,128)(2,1)}), bf16[16,2,2048]{2,1,0:T(2,128)(2,1)S(1)}, u32[]{:S(2)}, u32[]{:S(2)}) %all-to-all-start) | async-done | bytes 131104 | tf_op jit(solution)/shard_map/all_to_all | solution.py:21
  51.5 1.8 %reshape.9 = bf16[4096,1,16]{2,1,0:T(2,128)(2,1)S(1)} reshape(bf16[16,2,2048]{2,1,0:T(2,128)(2,1)S(1)} %all-to-all-done) | data formatting | bytes 262144
  53.3 0.0 copy-start
  53.3 2.0 %copy.9 = bf16[1,16,4096]{2,1,0:T(8,128)(2,1)S(1)} copy(bf16[1,16,4096]{1,0,2:T(2,128)(2,1)S(1)} %bitcast.26) | data formatting | bytes 262144 | tf_op jit(solution)/shard_map/all_to_all | solution.py:21
  55.3 0.3 multiply_reduce_fusion
  55.6 37.5 %psum.7 = f32[16]{0:T(128)S(1)} all-reduce(f32[16]{0:T(128)S(1)} %get-tuple-element.8), channel_id=1, replica_groups=mesh['path'=16,'shard'=2] {'path','shard'}, use_global_device_ids=true, to_apply=%region_2.3 | all-reduce | flops 16 | bytes 128 | tf_op jit(solution)/shard_map/psum | solution.py:30
  93.1 0.0 copy-done
  93.1 0.9 fusion
  94.0 0.0 all-gather.2.cloned.1.call-update
  94.0 0.6 dynamic_slice.8
  96.5 0.9 copy.12
  97.4 38.6 %all-gather.2.cloned.1.call-done = bf16[16,16,4096]{2,0,1:T(8,128)(2,1)} async-done(((bf16[16,16,256]{2,0,1:T(8,128)(2,1)}), bf16[16,16,4096]{2,0,1:T(8,128)(2,1)}) %all-gather.2.cloned.1.call-update) | async-done | bytes 2097168 | tf_op jit(solution)/shard_map/all_gather | solution.py:36
  136.0 1.5 %constant_dynamic-slice_fusion = bf16[1,16,4096]{2,0,1:T(2,128)(2,1)S(1)} fusion(bf16[16,16,4096]{2,0,1:T(8,128)(2,1)} %all-gather.2.cloned.1.call-done, s32[]{:T(128)S(6)} %select_n.9), kind=kLoop, calls=%fused_computation.12 | loop fusion | bytes 262148 | tf_op jit(solution)/shard_map/jit(dynamic_index_in_dim)/dynamic_slice | solution.py:37
  137.5 0.8 copy.11
  (2 shorter events, 0.0 us)
Async XLA Ops:
  12.0 31.6 %copy-start.1 = (s32[16]{0:T(128)S(1)}, s32[16]{0:T(128)}, u32[]{:S(2)}) copy-start(s32[16]{0:T(128)} %param.5) | copy-start | bytes 196
  36.2 15.3 %all-to-all-start = ((bf16[16,2,2048]{2,1,0:T(2,128)(2,1)}), bf16[16,2,2048]{2,1,0:T(2,128)(2,1)S(1)}, u32[]{:S(2)}, u32[]{:S(2)}) async-start(bf16[16,2,2048]{2,1,0:T(2,128)(2,1)} %reshape.8), calls=%async_computation | async-start | bytes 262144 | tf_op jit(solution)/shard_map/all_to_all | solution.py:21
  43.6 92.4 %all-gather.2.cloned.1.call-start = ((), (), s32[]{:S(2)}) async-start(), calls=%async_computation.1 | async-start | bytes 2228224 | tf_op jit(solution)/shard_map/all_gather | solution.py:36
  53.3 39.8 %copy-start = (f32[16,16,256]{2,1,0:T(8,128)S(1)}, f32[16,16,256]{2,1,0:T(8,128)}, u32[]{:S(2)}) copy-start(f32[16,16,256]{2,1,0:T(8,128)} %param.4) | copy-start | bytes 786436
Sparse Core Ops, SparseCore 0:
  94.1 41.7 all-gather.1
where the time goes:
time: 146 us; the launch traced here: 145 us
  waiting for transfers between devices  46.3 us (32%)
  blocking collectives  37.5 us (26%)
  other arithmetic  23.4 us (16%)
  between operations  16 us (11%)
  local copies, waits for them, and re-layouts  14.2 us (10%)
  starting transfers between devices  7.43 us (5%)
    all_gather x1, waiting for transfers between devices, local(): gathered = lax.all_gather(outer_step, 'path', axis=2, tiled=True)  38.6 us
    psum x1, blocking collectives, local(): norm_squares = lax.psum(local_squares, ('path', 'shard'))  37.5 us
    unnamed x1, other arithmetic  22.4 us
    unnamed x11, local copies, waits for them, and re-layouts  10.1 us
    all_to_all x1, waiting for transfers between devices, local(): lax.all_to_all(deltas, 'path', split_axis=2, concat_axis=0, tiled=True)  7.73 us
    all_to_all x1, starting transfers between devices, local(): lax.all_to_all(deltas, 'path', split_axis=2, concat_axis=0, tiled=True)  7.39 us
  transfers between devices with their start and end apart: 2, of which 2 were waited for; matrix products, arithmetic and copies ran while one was open for 1% of the time, Pallas kernels for 0%

commit v1 on v0

--- a/solution.py
+++ b/solution.py
@@ -18,7 +18,12 @@
     )
     counts = jnp.sum(onehot, axis=0)
     own_module = lax.dynamic_index_in_dim(path_module, own_index, 0, keepdims=False)
-    column_pieces = lax.all_to_all(deltas, "path", split_axis=2, concat_axis=0, tiled=True)
+    column_pieces = jnp.concatenate(
+        lax.all_to_all(
+            jnp.stack(jnp.split(deltas, lax.axis_size("path"), 2), axis=0), "path", 0, 0
+        ),
+        0,
+    )
     totals = jnp.einsum(
         "pm,prc->mrc",
         onehot.astype(jnp.bfloat16),

time: 146 us -> 136 us (0.932)
  other arithmetic: 23.4 us -> 2.59 us
  local copies, waits for them, and re-layouts: 14.2 us -> 24.5 us
    unnamed x1 -> x0, other arithmetic: 22.4 us -> none
    unnamed x11 -> x19, local copies, waits for them, and re-layouts: 10.1 us -> 21.1 us
    all_to_all x1 -> x0, local copies, waits for them, and re-layouts: 1.99 us -> none  [local(): lax.all_to_all(deltas, 'path', split_axis=2, concat_axis=0, tiled=True)]
  transfers between devices with their start and end apart: 2 -> 2, of which waited for: 2 -> 2; matrix products, arithmetic and copies ran while one was open for 1% -> 2% of each run, Pallas kernels for 0% -> 0%
where the time goes in v1:
time: 136 us; the launch traced here: 135 us
  waiting for transfers between devices  45.7 us (34%)
  blocking collectives  37.5 us (28%)
  local copies, waits for them, and re-layouts  24.5 us (18%)
  between operations  16 us (12%)
  starting transfers between devices  7.43 us (5%)
  other arithmetic  2.59 us (2%)
    all_gather x1, waiting for transfers between devices, local(): gathered = lax.all_gather(outer_step, 'path', axis=2, tiled=True)  38.6 us
    psum x1, blocking collectives, local(): norm_squares = lax.psum(local_squares, ('path', 'shard'))  37.5 us
    unnamed x19, local copies, waits for them, and re-layouts  21.1 us
    all_to_all x1, starting transfers between devices, local(): lax.all_to_all(jnp.stack(jnp.split(deltas, lax.axis_size('path'), 2), axi...  7.39 us
    all_to_all x1, waiting for transfers between devices, local(): lax.all_to_all(jnp.stack(jnp.split(deltas, lax.axis_size('path'), 2), axi...  7.08 us
  transfers between devices with their start and end apart: 2, of which 2 were waited for; matrix products, arithmetic and copies ran while one was open for 2% of the time, Pallas kernels for 0%

profile of v1, /device:TPU:0, one launch (start us, length us, event | category | flops | bytes accessed | tf_op | source)
XLA Modules:
  0.0 134.6 jit_solution(11604103474847722523)
XLA Ops:
  7.2 0.0 copy-start
  7.2 1.3 constant_dynamic-update-slice_fusion.15
  8.5 1.3 constant_dynamic-update-slice_fusion.14
  9.8 1.3 constant_dynamic-update-slice_fusion.13
  11.1 1.3 constant_dynamic-update-slice_fusion.12
  12.4 1.3 constant_dynamic-update-slice_fusion.11
  13.7 1.3 constant_dynamic-update-slice_fusion.10
  15.0 1.3 constant_dynamic-update-slice_fusion.9
  16.2 1.3 constant_dynamic-update-slice_fusion.8
  17.5 1.3 constant_dynamic-update-slice_fusion.7
  18.8 1.3 constant_dynamic-update-slice_fusion.6
  20.1 1.3 constant_dynamic-update-slice_fusion.5
  21.4 1.3 constant_dynamic-update-slice_fusion.4
  22.7 1.3 constant_dynamic-update-slice_fusion.3
  24.0 1.3 constant_dynamic-update-slice_fusion.2
  25.3 1.3 constant_dynamic-update-slice_fusion.1
  26.6 1.3 constant_dynamic-update-slice_fusion
  27.9 7.4 %all-to-all-start = ((bf16[16,1,16,256]{3,2,1,0:T(8,128)(2,1)}), bf16[16,1,16,256]{3,2,1,0:T(8,128)(2,1)S(1)}, u32[]{:S(2)}, u32[]{:S(2)}) async-start(bf16[16,1,16,256]{3,2,1,0:T(8,128)(2,1)} %constant_dynamic-update-slice_fusion), calls=%async_computation | async-start | bytes 262144 | tf_op jit(solution)/shard_map/all_to_all | solution.py:22
  35.3 0.0 all-gather.2.cloned.1.call-start
  35.3 0.8 convert_reduce_fusion
  36.1 7.1 %all-to-all-done = bf16[16,1,16,256]{3,2,1,0:T(8,128)(2,1)S(1)} async-done(((bf16[16,1,16,256]{3,2,1,0:T(8,128)(2,1)}), bf16[16,1,16,256]{3,2,1,0:T(8,128)(2,1)S(1)}, u32[]{:S(2)}, u32[]{:S(2)}) %all-to-all-start) | async-done | bytes 131104 | tf_op jit(solution)/shard_map/all_to_all | solution.py:22
  43.2 0.9 multiply_reduce_fusion
  44.1 37.5 %psum.7 = f32[16]{0:T(128)S(1)} all-reduce(f32[16]{0:T(128)S(1)} %get-tuple-element.10), channel_id=1, replica_groups=mesh['path'=16,'shard'=2] {'path','shard'}, use_global_device_ids=true, to_apply=%region_2.3 | all-reduce | flops 16 | bytes 128 | tf_op jit(solution)/shard_map/psum | solution.py:35
  81.6 1.8 %fusion = (f32[16,16,256]{2,0,1:T(8,128)S(1)}, bf16[16,16,256]{2,0,1:T(8,128)(2,1)}) fusion(f32[16,16,256]{2,1,0:T(8,128)} %param.4, f32[16,16,256]{2,0,1:T(8,128)S(1)} %get-tuple-element.11, f32[16]{0:T(128)S(1)} %multiply_minimum_fusion), kind=kLoop, calls=%fused_computation.2 | loop fusion | flops 458752 | bytes 917568 | tf_op jit(solution)/shard_map/add | solution.py:39
  83.4 0.0 all-gather.2.cloned.1.call-update
  83.5 0.0 copy-done
  83.5 0.6 dynamic_slice.8
  86.0 0.9 copy.30
  86.9 38.6 %all-gather.2.cloned.1.call-done = bf16[16,16,4096]{2,0,1:T(8,128)(2,1)} async-done(((bf16[16,16,256]{2,0,1:T(8,128)(2,1)}), bf16[16,16,4096]{2,0,1:T(8,128)(2,1)}) %all-gather.2.cloned.1.call-update) | async-done | bytes 2097168 | tf_op jit(solution)/shard_map/all_gather | solution.py:41
  125.4 1.5 %constant_dynamic-slice_fusion = bf16[1,16,4096]{2,0,1:T(2,128)(2,1)S(1)} fusion(bf16[16,16,4096]{2,0,1:T(8,128)(2,1)} %all-gather.2.cloned.1.call-done, s32[]{:T(128)S(6)} %select_n.9), kind=kLoop, calls=%fused_computation.29 | loop fusion | bytes 262148 | tf_op jit(solution)/shard_map/jit(dynamic_index_in_dim)/dynamic_slice | solution.py:42
  127.0 0.8 copy.29
  (1 shorter events, 0.0 us)
Async XLA Ops:
  7.2 76.3 %copy-start = (s32[16]{0:T(128)S(1)}, s32[16]{0:T(128)}, u32[]{:S(2)}) copy-start(s32[16]{0:T(128)} %param.5) | copy-start | bytes 196
  27.9 15.3 %all-to-all-start = ((bf16[16,1,16,256]{3,2,1,0:T(8,128)(2,1)}), bf16[16,1,16,256]{3,2,1,0:T(8,128)(2,1)S(1)}, u32[]{:S(2)}, u32[]{:S(2)}) async-start(bf16[16,1,16,256]{3,2,1,0:T(8,128)(2,1)} %constant_dynamic-update-slice_fusion), calls=%async_computation | async-start | bytes 262144 | tf_op jit(solution)/shard_map/all_to_all | solution.py:22
  35.3 90.1 %all-gather.2.cloned.1.call-start = ((), (), s32[]{:S(2)}) async-start(), calls=%async_computation.1 | async-start | bytes 2228224 | tf_op jit(solution)/shard_map/all_gather | solution.py:41
Sparse Core Ops, SparseCore 0:
  83.6 41.7 all-gather.1
